TPU v7x, 32 devices: a whole 2x2x4 slice. The times are simulated.
32 devices in a mesh: section: 2 (over x), tp: 16 (over z, y, core).
Axes of the slice: x: 2, y: 2, z: 4, core: 2. Of those that a mesh axis runs over, the one named last changes fastest.
Arguments:
- states: float32 [2, 128, 4096], P('section', 'tp'), may hold values from -6 to 6
- text_embed: bfloat16 [1, 128, 4096], P(None, 'tp'), may hold values from -6 to 6
- visual_embed: bfloat16 [1, 128, 4096], P(None, 'tp'), may hold values from -6 to 6
- prefix_len: int32 [1, 4], replicated, may hold values from 1 to 31
- segment_ids: int32 [3, 128], replicated, may hold values from 0 to 3, never falling along the last dimension, each value on 1 to 64 neighbouring positions
- gain: float32 [2, 4096], P('section'), may hold values from 0.25 to 1.75
- w_query: bfloat16 [2, 4096, 2048], P('section', None, 'tp'), may hold values from -0.5625 to 0.5625
- w_keyval: bfloat16 [2, 4096, 2048], P('section', None, 'tp'), may hold values from -0.5625 to 0.5625
- w_out: bfloat16 [2, 2048, 4096], P('section', 'tp'), may hold values from -0.5 to 0.5
Outputs:
- section_out: float32 [2, 2, 128, 4096], P(None, 'section', 'tp')
All inputs are finite; a program needn't handle non-finite values.
Results may differ from a plain program's by a relative error of at most 0.028.
Values may be sent and summed in bfloat16 or wider, within the bound.
A program may use at most 64 MiB of HBM per device.

v0:
```python
import jax
import jax.numpy as jnp
from jax import lax
from jax.sharding import PartitionSpec as P

HEAD = 64
WINDOW = 2
norm_eps = 1e-05
rope_base = 500000.0


def shifted(block, axis, distance):
    devices = range(lax.axis_size(axis))
    route = [(i - distance, i) for i in devices if i - distance in devices]
    return lax.ppermute(block, axis, route)


def seg_offsets(seg_row):
    earlier = (seg_row[None, :] < seg_row[:, None]).astype(jnp.int32)
    first_pos = jnp.sum(earlier, axis=1)
    return jnp.arange(seg_row.shape[0], dtype=jnp.int32) - first_pos


def rotate(values, offsets):
    half_dim = values.shape[-1] // 2
    inv_freq = rope_base ** (-(jnp.arange(half_dim, dtype=jnp.float32) * 2.0) / values.shape[-1])
    angles = offsets.astype(jnp.float32)[:, None] * inv_freq[None, :]
    view_shape = (values.shape[0],) + (1,) * (values.ndim - 2) + (half_dim,)
    cosine = jnp.cos(angles).reshape(view_shape)
    sine_part = jnp.sin(angles).reshape(view_shape)
    front_half = values[..., :half_dim]
    back_half = values[..., half_dim:]
    return jnp.concatenate(
        [front_half * cosine - back_half * sine_part, back_half * cosine + front_half * sine_part],
        axis=-1,
    )


def rms_normed(rows, gain_row):
    scale = lax.rsqrt(jnp.mean(rows * rows, axis=-1, keepdims=True) + norm_eps)
    return rows * scale * gain_row


def body(states, text_embed, visual_embed, prefix_len, segment_ids, gain, w_query, w_keyval, w_out):
    section_pos = lax.axis_index("section")
    rank_pos = lax.axis_index("tp")
    section_count = lax.axis_size("section")
    shard_rows = states.shape[1]
    gain_row = gain[0]
    query_w = w_query[0]
    keyval_w = w_keyval[0]
    out_w = w_out[0]
    query_cols = query_w.shape[1]
    residual = states[0]
    outputs = []
    for step_num in range(WINDOW):
        if step_num > 0:
            arrived = shifted(residual.astype(jnp.bfloat16), "section", 1).astype(residual.dtype)
            batch_num = step_num - 1
            embed_seg_row = segment_ids[section_count + batch_num]
            offsets = seg_offsets(embed_seg_row)
            onehot = (
                embed_seg_row[:, None] == jnp.arange(prefix_len.shape[1], dtype=jnp.int32)[None, :]
            )
            prefix_cap = jnp.sum(jnp.where(onehot, prefix_len[batch_num][None, :], 0), axis=1)
            own_visual = lax.dynamic_slice_in_dim(
                offsets < prefix_cap, rank_pos * shard_rows, shard_rows, 0
            )
            residual = jnp.where(
                section_pos == 0,
                jnp.where(
                    own_visual[:, None], visual_embed[batch_num], text_embed[batch_num]
                ).astype(jnp.float32),
                arrived,
            )
        seg_row = lax.dynamic_index_in_dim(
            segment_ids, step_num - section_pos + section_count - 1, 0, keepdims=False
        )
        apply_normed = rms_normed(residual, gain_row).astype(jnp.bfloat16)
        normed = lax.all_gather(apply_normed, "tp", axis=0, tiled=True)
        mapped = jnp.concatenate(
            [
                jnp.dot(normed, query_w, preferred_element_type=jnp.float32),
                jnp.dot(normed, keyval_w, preferred_element_type=jnp.float32),
            ],
            axis=1,
        )
        total_rows = mapped.shape[0]
        apply_offsets = seg_offsets(seg_row)
        queries = rotate(
            mapped[:, :query_cols].reshape(total_rows, query_cols // HEAD, HEAD), apply_offsets
        ).astype(jnp.bfloat16)
        key_rows = rotate(mapped[:, query_cols : query_cols + HEAD], apply_offsets).astype(
            jnp.bfloat16
        )
        value_rows = mapped[:, query_cols + HEAD :].astype(jnp.bfloat16)
        scores = jnp.einsum(
            "qhd,kd->hqk", queries, key_rows, preferred_element_type=jnp.float32
        ) * HEAD ** (-0.5)
        position = jnp.arange(total_rows, dtype=jnp.int32)
        allowed = (seg_row[None, :] == seg_row[:, None]) & (position[None, :] <= position[:, None])
        scores = jnp.where(allowed[None], scores, -1e30)
        weights = jax.nn.softmax(scores, axis=-1).astype(jnp.bfloat16)
        mixed_heads = (
            jnp.einsum("hqk,kd->qhd", weights, value_rows, preferred_element_type=jnp.float32)
            .astype(jnp.bfloat16)
            .reshape(total_rows, query_cols)
        )
        residual = residual + lax.psum_scatter(
            jnp.dot(mixed_heads, out_w, preferred_element_type=jnp.float32).astype(jnp.bfloat16),
            "tp",
            scatter_dimension=0,
            tiled=True,
        ).astype(jnp.float32)
        outputs.append(residual)
    return jnp.stack(outputs)[:, None]


def solution(mesh):
    return jax.shard_map(
        body,
        mesh=mesh,
        in_specs=(
            P("section", "tp", None),
            P(None, "tp", None),
            P(None, "tp", None),
            P(),
            P(),
            P("section", None),
            P("section", None, "tp"),
            P("section", None, "tp"),
            P("section", "tp", None),
        ),
        out_specs=P(None, "section", "tp", None),
        check_vma=False,
    )
```

profile of v0, /device:TPU:0, one launch (start us, length us, event | category | flops | bytes accessed | tf_op | source)
XLA Modules:
  0.0 227.0 jit_solution(10462846901884635893)
XLA Ops:
  6.5 1.1 fusion.20
  7.7 1.6 fusion.22
  9.3 0.0 all-gather.3.cloned.1.call-update
  9.3 0.0 reduce-scatter.3.cloned.1.call-start
  9.4 0.0 copy-start.10
  9.4 0.0 copy-start.1
  9.4 1.6 copy.19
  11.0 0.6 slice_bitcast_fusion
  11.6 0.1 convert_reduce_fusion.2
  11.7 0.1 fusion.26
  11.8 38.3 %all-gather.3.cloned.1.call-done = bf16[128,4096]{1,0:T(8,128)(2,1)} async-done(((bf16[8,4096]{1,0:T(8,128)(2,1)}), bf16[128,4096]{1,0:T(8,128)(2,1)}) %all-gather.3.cloned.1.call-update) | async-done | bytes 1048592 | tf_op jit(solution)/shard_map/all_gather | solution.py:80
  50.1 1.8 fusion.18
  51.9 0.1 subtract_convert_fusion.3
  52.1 0.5 fusion.14
  52.7 0.2 fusion.57
  52.9 0.2 fusion.9
  53.1 0.2 convolution_convert_fusion.3
  53.3 0.0 copy-done
  53.3 1.5 convolution_convert_fusion.1
  54.8 0.0 reduce-scatter.3.cloned.1.call-update
  54.8 0.0 all-gather.5.cloned.1.call-start
  54.9 0.6 copy-done.11
  55.4 0.7 convert_reduce_fusion.1
  56.1 0.7 select_reduce_fusion
  56.8 54.8 %reduce-scatter.3.cloned.1.call-done = bf16[8,4096]{1,0:T(8,128)(2,1)} async-done(((bf16[128,4096]{1,0:T(8,128)(2,1)}), bf16[8,4096]{1,0:T(8,128)(2,1)}) %reduce-scatter.3.cloned.1.call-update) | async-done | bytes 65552 | tf_op jit(solution)/shard_map/reduce_scatter | solution.py:109
  111.6 1.5 fusion.24
  113.1 3.3 %collective-permute-start = (bf16[8,4096]{1,0:T(8,128)(2,1)}, bf16[8,4096]{1,0:T(8,128)(2,1)S(1)}, u32[]{:S(2)}, u32[]{:S(2)}) collective-permute-start(bf16[8,4096]{1,0:T(8,128)(2,1)} %get-tuple-element.8), channel_id=1, source_target_pairs={{0,16},{1,17},{2,18},{3,19},{4,20},{5,21},{6,22},{7,23},{8,24},{9,... | collective-permute-start | bytes 196616 | tf_op jit(solution)/shard_map/ppermute | solution.py:15
  116.4 0.7 subtract_compare_fusion
  117.1 0.1 dynamic_slice.16
  117.2 1.4 collective-permute-done
  118.6 0.2 multiply_reduce_fusion
  118.9 0.7 multiply_convert_fusion
  119.6 0.0 all-gather.5.cloned.1.call-update
  119.6 0.0 reduce-scatter.5.cloned.1.call-start
  119.7 0.8 convert_reduce_fusion
  120.5 0.8 fusion.25
  121.3 36.1 %all-gather.5.cloned.1.call-done = bf16[128,4096]{1,0:T(8,128)(2,1)} async-done(((bf16[8,4096]{1,0:T(8,128)(2,1)}), bf16[128,4096]{1,0:T(8,128)(2,1)}) %all-gather.5.cloned.1.call-update) | async-done | bytes 1048592 | tf_op jit(solution)/shard_map/all_gather | solution.py:80
  157.4 1.8 fusion.16
  159.3 0.1 subtract_convert_fusion.2
  159.4 0.5 fusion.10
  160.0 0.2 fusion.60
  160.2 0.2 fusion.7
  160.4 0.2 convolution_convert_fusion.2
  160.6 1.5 convolution_convert_fusion
  162.1 0.0 reduce-scatter.5.cloned.1.call-update
  162.1 56.8 %reduce-scatter.5.cloned.1.call-done = bf16[8,4096]{1,0:T(8,128)(2,1)} async-done(((bf16[128,4096]{1,0:T(8,128)(2,1)}), bf16[8,4096]{1,0:T(8,128)(2,1)}) %reduce-scatter.5.cloned.1.call-update) | async-done | bytes 65552 | tf_op jit(solution)/shard_map/reduce_scatter | solution.py:109
  218.9 0.9 add_bitcast_fusion
  219.7 0.7 maximum_bitcast_fusion
  (30 shorter events, 0.1 us)
Async XLA Ops:
  6.5 46.8 %copy-start = (bf16[1,128,4096]{2,1,0:T(8,128)(2,1)S(1)}, bf16[1,128,4096]{2,1,0:T(8,128)(2,1)}, u32[]{:S(2)}) copy-start(bf16[1,128,4096]{2,1,0:T(8,128)(2,1)} %param.17) | copy-start | bytes 3145732
  6.5 43.6 %all-gather.3.cloned.1.call-start = ((), (), s32[]{:S(2)}) async-start(), calls=%async_computation.2 | async-start | bytes 1114112 | tf_op jit(solution)/shard_map/all_gather | solution.py:80
  9.3 102.3 %reduce-scatter.3.cloned.1.call-start = ((), (), s32[]{:S(2)}) async-start(), calls=%async_computation.3 | async-start | bytes 1114112 | tf_op jit(solution)/shard_map/reduce_scatter | solution.py:109
  9.4 1.6 copy-start.10
  9.4 40.7 %copy-start.1 = (bf16[1,4096,128]{2,1,0:T(8,128)(2,1)S(1)}, bf16[1,4096,128]{2,1,0:T(8,128)(2,1)}, u32[]{:S(2)}) copy-start(bf16[1,4096,128]{2,1,0:T(8,128)(2,1)} %param.16) | copy-start | bytes 3145732
  11.0 40.9 %copy-start.8 = (f32[32]{0:T(128)}, f32[32]{0:T(128)S(1)}, u32[]{:S(2)}) copy-start(f32[32]{0:T(128)S(1)} %multiply_power_fusion) | copy-start | bytes 388
  50.1 2.0 copy-start.2
  54.8 0.7 copy-start.11
  54.8 1.4 copy-start.12
  54.8 56.9 %copy-start.4 = (f32[1,8,4096]{2,1,0:T(8,128)S(1)}, f32[1,8,4096]{2,1,0:T(8,128)}, u32[]{:S(2)}) copy-start(f32[1,8,4096]{2,1,0:T(8,128)} %param.9) | copy-start | bytes 393220
  54.8 63.8 %copy-start.5 = (bf16[1,8,4096]{2,1,0:T(8,128)(2,1)S(1)}, bf16[1,8,4096]{2,1,0:T(8,128)(2,1)}, u32[]{:S(2)}) copy-start(bf16[1,8,4096]{2,1,0:T(8,128)(2,1)} %param.10) | copy-start | bytes 196612
  54.8 63.8 %copy-start.6 = (bf16[1,8,4096]{2,1,0:T(8,128)(2,1)S(1)}, bf16[1,8,4096]{2,1,0:T(8,128)(2,1)}, u32[]{:S(2)}) copy-start(bf16[1,8,4096]{2,1,0:T(8,128)(2,1)} %param.11) | copy-start | bytes 196612
  54.8 64.1 %copy-start.7 = (f32[1,4096]{1,0:T(1,128)S(1)}, f32[1,4096]{1,0:T(1,128)}, u32[]{:S(2)}) copy-start(f32[1,4096]{1,0:T(1,128)} %param.14) | copy-start | bytes 49156
  54.8 102.6 %all-gather.5.cloned.1.call-start = ((), (), s32[]{:S(2)}) async-start(), calls=%async_computation.4 | async-start | bytes 1114112 | tf_op jit(solution)/shard_map/all_gather | solution.py:80
  113.1 5.5 %collective-permute-start = (bf16[8,4096]{1,0:T(8,128)(2,1)}, bf16[8,4096]{1,0:T(8,128)(2,1)S(1)}, u32[]{:S(2)}, u32[]{:S(2)}) collective-permute-start(bf16[8,4096]{1,0:T(8,128)(2,1)} %get-tuple-element.8), channel_id=1, source_target_pairs={{0,16},{1,17},{2,18},{3,19},{4,20},{5,21},{6,22},{7,23},{8,24},{9,... | collective-permute-start | bytes 196616 | tf_op jit(solution)/shard_map/ppermute | solution.py:15
  119.6 99.2 %reduce-scatter.5.cloned.1.call-start = ((), (), s32[]{:S(2)}) async-start(), calls=%async_computation.5 | async-start | bytes 1114112 | tf_op jit(solution)/shard_map/reduce_scatter | solution.py:109
  121.3 37.9 %copy-start.9 = (f32[32]{0:T(128)S(1)}, f32[32]{0:T(128)}, u32[]{:S(2)}) copy-start(f32[32]{0:T(128)} %copy-done.8) | copy-start | bytes 388
  157.4 2.0 copy-start.3
Sparse Core Ops, SparseCore 0:
  9.5 40.5 all-gather.2
  54.9 56.6 reduce-scatter.2
  119.7 37.6 all-gather.4
  162.2 56.5 reduce-scatter.4
where the time goes:
time: 227 us
  waiting for transfers between devices  187 us (82%)
  between operations  13.3 us (6%)
  other arithmetic  11 us (5%)
  matrix products  8.88 us (4%)
  starting transfers between devices  3.4 us (1%)
  local copies, waits for them, and re-layouts  2.86 us (1%)
    reduce_scatter x2, waiting for transfers between devices, body(): lax.psum_scatter(jnp.dot(mixed_heads, out_w, preferred_element_type=jnp.f...  112 us
    all_gather x2, waiting for transfers between devices, body(): normed = lax.all_gather(apply_normed, 'tp', axis=0, tiled=True)  74.3 us
  transfers between devices with their start and end apart: 5, of which 5 were waited for; matrix products, arithmetic and copies ran while one was open for 3% of the time, Pallas kernels for 0%

commit v1 on v0

--- a/solution.py
+++ b/solution.py
@@ -77,7 +77,25 @@
             segment_ids, step_num - section_pos + section_count - 1, 0, keepdims=False
         )
         apply_normed = rms_normed(residual, gain_row).astype(jnp.bfloat16)
-        normed = lax.all_gather(apply_normed, "tp", axis=0, tiled=True)
+
+        def field_see(vec):
+            xs_all = [vec]
+            how_many = jax.lax.axis_size("tp")
+            d = 0
+            while d < how_many - 1:
+                xs_all.append(
+                    jax.lax.ppermute(
+                        xs_all[-1],
+                        "tp",
+                        [(dev_i, (dev_i + 1) % how_many) for dev_i in range(how_many)],
+                    )
+                )
+                d += 1
+            return jnp.roll(
+                jnp.concatenate(xs_all[::-1], 0), (jax.lax.axis_index("tp") + 1) * vec.shape[0], 0
+            )
+
+        normed = field_see(apply_normed)
         mapped = jnp.concatenate(
             [
                 jnp.dot(normed, query_w, preferred_element_type=jnp.float32),

time: 227 us -> 337 us (1.48)
  waiting for transfers between devices: 187 us -> 302 us
  other arithmetic: 11 us -> 5.98 us
    ppermute x0 -> x30, waiting for transfers between devices: none -> 189 us  [field_see(): jax.lax.ppermute(xs_all[-1], 'tp', [(dev_i, (dev_i + 1) % how_many) for d...]
    all_gather x2 -> x0, waiting for transfers between devices: 74.3 us -> none  [body(): normed = lax.all_gather(apply_normed, 'tp', axis=0, tiled=True)]
  transfers between devices with their start and end apart: 5 -> 33, of which waited for: 5 -> 33; matrix products, arithmetic and copies ran while one was open for 3% -> 1% of each run, Pallas kernels for 0% -> 0%
where the time goes in v1:
time: 337 us
  waiting for transfers between devices  302 us (90%)
  between operations  13.9 us (4%)
  matrix products  7.3 us (2%)
  other arithmetic  5.98 us (2%)
  starting transfers between devices  4.17 us (1%)
  local copies, waits for them, and re-layouts  3.91 us (1%)
    ppermute x30, waiting for transfers between devices, field_see(): jax.lax.ppermute(xs_all[-1], 'tp', [(dev_i, (dev_i + 1) % how_many) for d...  189 us
    reduce_scatter x2, waiting for transfers between devices, body(): lax.psum_scatter(jnp.dot(mixed_heads, out_w, preferred_element_type=jnp.f...  111 us
  transfers between devices with their start and end apart: 33, of which 33 were waited for; matrix products, arithmetic and copies ran while one was open for 1% of the time, Pallas kernels for 0%

profile of v1, /device:TPU:0, one launch (start us, length us, event | category | flops | bytes accessed | tf_op | source)
XLA Modules:
  0.0 337.0 jit_solution(17197074370112051363)
XLA Ops:
  6.5 1.1 fusion.22
  7.7 1.0 fusion.24
  9.2 6.9 %collective-permute-done = bf16[8,4096]{1,0:T(8,128)(2,1)S(1)} collective-permute-done((bf16[8,4096]{1,0:T(8,128)(2,1)S(1)}, bf16[8,4096]{1,0:T(8,128)(2,1)S(1)}, u32[]{:S(2)}, u32[]{:S(2)}) %collective-permute-start) | collective-permute-done | bytes 65568 | tf_op jit(solution)/shard_map/ppermute | solution.py:87
  16.2 6.4 %collective-permute-done.1 = bf16[8,4096]{1,0:T(8,128)(2,1)S(1)} collective-permute-done((bf16[8,4096]{1,0:T(8,128)(2,1)S(1)}, bf16[8,4096]{1,0:T(8,128)(2,1)S(1)}, u32[]{:S(2)}, u32[]{:S(2)}) %collective-permute-start.1) | collective-permute-done | bytes 65568 | tf_op jit(solution)/shard_map/ppermute | solution.py:87
  22.6 6.4 %collective-permute-done.2 = bf16[8,4096]{1,0:T(8,128)(2,1)S(1)} collective-permute-done((bf16[8,4096]{1,0:T(8,128)(2,1)S(1)}, bf16[8,4096]{1,0:T(8,128)(2,1)S(1)}, u32[]{:S(2)}, u32[]{:S(2)}) %collective-permute-start.2) | collective-permute-done | bytes 65568 | tf_op jit(solution)/shard_map/ppermute | solution.py:87
  28.9 6.4 %collective-permute-done.3 = bf16[8,4096]{1,0:T(8,128)(2,1)S(1)} collective-permute-done((bf16[8,4096]{1,0:T(8,128)(2,1)S(1)}, bf16[8,4096]{1,0:T(8,128)(2,1)S(1)}, u32[]{:S(2)}, u32[]{:S(2)}) %collective-permute-start.3) | collective-permute-done | bytes 65568 | tf_op jit(solution)/shard_map/ppermute | solution.py:87
  35.3 6.4 %collective-permute-done.4 = bf16[8,4096]{1,0:T(8,128)(2,1)S(1)} collective-permute-done((bf16[8,4096]{1,0:T(8,128)(2,1)S(1)}, bf16[8,4096]{1,0:T(8,128)(2,1)S(1)}, u32[]{:S(2)}, u32[]{:S(2)}) %collective-permute-start.4) | collective-permute-done | bytes 65568 | tf_op jit(solution)/shard_map/ppermute | solution.py:87
  41.7 6.4 %collective-permute-done.5 = bf16[8,4096]{1,0:T(8,128)(2,1)S(1)} collective-permute-done((bf16[8,4096]{1,0:T(8,128)(2,1)S(1)}, bf16[8,4096]{1,0:T(8,128)(2,1)S(1)}, u32[]{:S(2)}, u32[]{:S(2)}) %collective-permute-start.5) | collective-permute-done | bytes 65568 | tf_op jit(solution)/shard_map/ppermute | solution.py:87
  48.1 6.4 %collective-permute-done.6 = bf16[8,4096]{1,0:T(8,128)(2,1)S(1)} collective-permute-done((bf16[8,4096]{1,0:T(8,128)(2,1)S(1)}, bf16[8,4096]{1,0:T(8,128)(2,1)S(1)}, u32[]{:S(2)}, u32[]{:S(2)}) %collective-permute-start.6) | collective-permute-done | bytes 65568 | tf_op jit(solution)/shard_map/ppermute | solution.py:87
  54.5 6.4 %collective-permute-done.7 = bf16[8,4096]{1,0:T(8,128)(2,1)S(1)} collective-permute-done((bf16[8,4096]{1,0:T(8,128)(2,1)S(1)}, bf16[8,4096]{1,0:T(8,128)(2,1)S(1)}, u32[]{:S(2)}, u32[]{:S(2)}) %collective-permute-start.7) | collective-permute-done | bytes 65568 | tf_op jit(solution)/shard_map/ppermute | solution.py:87
  60.9 6.4 %collective-permute-done.8 = bf16[8,4096]{1,0:T(8,128)(2,1)S(1)} collective-permute-done((bf16[8,4096]{1,0:T(8,128)(2,1)S(1)}, bf16[8,4096]{1,0:T(8,128)(2,1)S(1)}, u32[]{:S(2)}, u32[]{:S(2)}) %collective-permute-start.8) | collective-permute-done | bytes 65568 | tf_op jit(solution)/shard_map/ppermute | solution.py:87
  67.3 6.4 %collective-permute-done.9 = bf16[8,4096]{1,0:T(8,128)(2,1)S(1)} collective-permute-done((bf16[8,4096]{1,0:T(8,128)(2,1)S(1)}, bf16[8,4096]{1,0:T(8,128)(2,1)S(1)}, u32[]{:S(2)}, u32[]{:S(2)}) %collective-permute-start.9) | collective-permute-done | bytes 65568 | tf_op jit(solution)/shard_map/ppermute | solution.py:87
  73.7 0.8 slice_bitcast_fusion
  74.5 5.6 %collective-permute-done.10 = bf16[8,4096]{1,0:T(8,128)(2,1)S(1)} collective-permute-done((bf16[8,4096]{1,0:T(8,128)(2,1)S(1)}, bf16[8,4096]{1,0:T(8,128)(2,1)S(1)}, u32[]{:S(2)}, u32[]{:S(2)}) %collective-permute-start.10) | collective-permute-done | bytes 65568 | tf_op jit(solution)/shard_map/ppermute | solution.py:87
  80.1 6.3 %collective-permute-done.11 = bf16[8,4096]{1,0:T(8,128)(2,1)S(1)} collective-permute-done((bf16[8,4096]{1,0:T(8,128)(2,1)S(1)}, bf16[8,4096]{1,0:T(8,128)(2,1)S(1)}, u32[]{:S(2)}, u32[]{:S(2)}) %collective-permute-start.11) | collective-permute-done | bytes 65568 | tf_op jit(solution)/shard_map/ppermute | solution.py:87
  86.5 6.3 %collective-permute-done.12 = bf16[8,4096]{1,0:T(8,128)(2,1)S(1)} collective-permute-done((bf16[8,4096]{1,0:T(8,128)(2,1)S(1)}, bf16[8,4096]{1,0:T(8,128)(2,1)S(1)}, u32[]{:S(2)}, u32[]{:S(2)}) %collective-permute-start.12) | collective-permute-done | bytes 65568 | tf_op jit(solution)/shard_map/ppermute | solution.py:87
  92.8 1.5 copy.19
  94.4 4.9 %collective-permute-done.13 = bf16[8,4096]{1,0:T(8,128)(2,1)S(1)} collective-permute-done((bf16[8,4096]{1,0:T(8,128)(2,1)S(1)}, bf16[8,4096]{1,0:T(8,128)(2,1)S(1)}, u32[]{:S(2)}, u32[]{:S(2)}) %collective-permute-start.13) | collective-permute-done | bytes 65568 | tf_op jit(solution)/shard_map/ppermute | solution.py:87
  99.2 6.4 %collective-permute-done.14 = bf16[8,4096]{1,0:T(8,128)(2,1)S(1)} collective-permute-done((bf16[8,4096]{1,0:T(8,128)(2,1)S(1)}, bf16[8,4096]{1,0:T(8,128)(2,1)S(1)}, u32[]{:S(2)}, u32[]{:S(2)}) %collective-permute-start.14) | collective-permute-done | bytes 65568 | tf_op jit(solution)/shard_map/ppermute | solution.py:87
  105.9 0.9 copy-done.5
  106.8 0.8 fusion.20
  107.6 0.8 fusion.16
  109.2 1.4 convolution_convert_fusion.1
  111.4 54.7 %reduce-scatter.3.cloned.1.call-done = bf16[8,4096]{1,0:T(8,128)(2,1)} async-done(((bf16[128,4096]{1,0:T(8,128)(2,1)}), bf16[8,4096]{1,0:T(8,128)(2,1)}) %reduce-scatter.3.cloned.1.call-update) | async-done | bytes 65552 | tf_op jit(solution)/shard_map/reduce_scatter | solution.py:127
  166.1 0.9 fusion.26
  167.0 3.5 %collective-permute-start.15 = (bf16[8,4096]{1,0:T(8,128)(2,1)S(1)}, bf16[8,4096]{1,0:T(8,128)(2,1)S(1)}, u32[]{:S(2)}, u32[]{:S(2)}) collective-permute-start(bf16[8,4096]{1,0:T(8,128)(2,1)S(1)} %get-tuple-element.9), channel_id=1, source_target_pairs={{0,16},{1,17},{2,18},{3,19},{4,20},{5,21},{6,22},{7,23},{8,24},{9,... | collective-permute-start | bytes 196616 | tf_op jit(solution)/shard_map/ppermute | solution.py:15
  170.5 1.8 collective-permute-done.15
  172.7 6.4 %collective-permute-done.16 = bf16[8,4096]{1,0:T(8,128)(2,1)S(1)} collective-permute-done((bf16[8,4096]{1,0:T(8,128)(2,1)S(1)}, bf16[8,4096]{1,0:T(8,128)(2,1)S(1)}, u32[]{:S(2)}, u32[]{:S(2)}) %collective-permute-start.16) | collective-permute-done | bytes 65568 | tf_op jit(solution)/shard_map/ppermute | solution.py:87
  179.1 6.4 %collective-permute-done.17 = bf16[8,4096]{1,0:T(8,128)(2,1)S(1)} collective-permute-done((bf16[8,4096]{1,0:T(8,128)(2,1)S(1)}, bf16[8,4096]{1,0:T(8,128)(2,1)S(1)}, u32[]{:S(2)}, u32[]{:S(2)}) %collective-permute-start.17) | collective-permute-done | bytes 65568 | tf_op jit(solution)/shard_map/ppermute | solution.py:87
  185.5 6.4 %collective-permute-done.18 = bf16[8,4096]{1,0:T(8,128)(2,1)S(1)} collective-permute-done((bf16[8,4096]{1,0:T(8,128)(2,1)S(1)}, bf16[8,4096]{1,0:T(8,128)(2,1)S(1)}, u32[]{:S(2)}, u32[]{:S(2)}) %collective-permute-start.18) | collective-permute-done | bytes 65568 | tf_op jit(solution)/shard_map/ppermute | solution.py:87
  191.9 6.4 %collective-permute-done.19 = bf16[8,4096]{1,0:T(8,128)(2,1)S(1)} collective-permute-done((bf16[8,4096]{1,0:T(8,128)(2,1)S(1)}, bf16[8,4096]{1,0:T(8,128)(2,1)S(1)}, u32[]{:S(2)}, u32[]{:S(2)}) %collective-permute-start.19) | collective-permute-done | bytes 65568 | tf_op jit(solution)/shard_map/ppermute | solution.py:87
  198.3 6.4 %collective-permute-done.20 = bf16[8,4096]{1,0:T(8,128)(2,1)S(1)} collective-permute-done((bf16[8,4096]{1,0:T(8,128)(2,1)S(1)}, bf16[8,4096]{1,0:T(8,128)(2,1)S(1)}, u32[]{:S(2)}, u32[]{:S(2)}) %collective-permute-start.20) | collective-permute-done | bytes 65568 | tf_op jit(solution)/shard_map/ppermute | solution.py:87
  204.6 6.4 %collective-permute-done.21 = bf16[8,4096]{1,0:T(8,128)(2,1)S(1)} collective-permute-done((bf16[8,4096]{1,0:T(8,128)(2,1)S(1)}, bf16[8,4096]{1,0:T(8,128)(2,1)S(1)}, u32[]{:S(2)}, u32[]{:S(2)}) %collective-permute-start.21) | collective-permute-done | bytes 65568 | tf_op jit(solution)/shard_map/ppermute | solution.py:87
  211.0 6.4 %collective-permute-done.22 = bf16[8,4096]{1,0:T(8,128)(2,1)S(1)} collective-permute-done((bf16[8,4096]{1,0:T(8,128)(2,1)S(1)}, bf16[8,4096]{1,0:T(8,128)(2,1)S(1)}, u32[]{:S(2)}, u32[]{:S(2)}) %collective-permute-start.22) | collective-permute-done | bytes 65568 | tf_op jit(solution)/shard_map/ppermute | solution.py:87
  217.4 6.4 %collective-permute-done.23 = bf16[8,4096]{1,0:T(8,128)(2,1)S(1)} collective-permute-done((bf16[8,4096]{1,0:T(8,128)(2,1)S(1)}, bf16[8,4096]{1,0:T(8,128)(2,1)S(1)}, u32[]{:S(2)}, u32[]{:S(2)}) %collective-permute-start.23) | collective-permute-done | bytes 65568 | tf_op jit(solution)/shard_map/ppermute | solution.py:87
  223.8 6.4 %collective-permute-done.24 = bf16[8,4096]{1,0:T(8,128)(2,1)S(1)} collective-permute-done((bf16[8,4096]{1,0:T(8,128)(2,1)S(1)}, bf16[8,4096]{1,0:T(8,128)(2,1)S(1)}, u32[]{:S(2)}, u32[]{:S(2)}) %collective-permute-start.24) | collective-permute-done | bytes 65568 | tf_op jit(solution)/shard_map/ppermute | solution.py:87
  230.2 6.4 %collective-permute-done.25 = bf16[8,4096]{1,0:T(8,128)(2,1)S(1)} collective-permute-done((bf16[8,4096]{1,0:T(8,128)(2,1)S(1)}, bf16[8,4096]{1,0:T(8,128)(2,1)S(1)}, u32[]{:S(2)}, u32[]{:S(2)}) %collective-permute-start.25) | collective-permute-done | bytes 65568 | tf_op jit(solution)/shard_map/ppermute | solution.py:87
  236.6 6.4 %collective-permute-done.26 = bf16[8,4096]{1,0:T(8,128)(2,1)S(1)} collective-permute-done((bf16[8,4096]{1,0:T(8,128)(2,1)S(1)}, bf16[8,4096]{1,0:T(8,128)(2,1)S(1)}, u32[]{:S(2)}, u32[]{:S(2)}) %collective-permute-start.26) | collective-permute-done | bytes 65568 | tf_op jit(solution)/shard_map/ppermute | solution.py:87
  243.0 6.4 %collective-permute-done.27 = bf16[8,4096]{1,0:T(8,128)(2,1)S(1)} collective-permute-done((bf16[8,4096]{1,0:T(8,128)(2,1)S(1)}, bf16[8,4096]{1,0:T(8,128)(2,1)S(1)}, u32[]{:S(2)}, u32[]{:S(2)}) %collective-permute-start.27) | collective-permute-done | bytes 65568 | tf_op jit(solution)/shard_map/ppermute | solution.py:87
  249.5 6.3 %collective-permute-done.28 = bf16[8,4096]{1,0:T(8,128)(2,1)S(1)} collective-permute-done((bf16[8,4096]{1,0:T(8,128)(2,1)S(1)}, bf16[8,4096]{1,0:T(8,128)(2,1)S(1)}, u32[]{:S(2)}, u32[]{:S(2)}) %collective-permute-start.28) | collective-permute-done | bytes 65568 | tf_op jit(solution)/shard_map/ppermute | solution.py:87
  255.8 6.3 %collective-permute-done.29 = bf16[8,4096]{1,0:T(8,128)(2,1)S(1)} collective-permute-done((bf16[8,4096]{1,0:T(8,128)(2,1)S(1)}, bf16[8,4096]{1,0:T(8,128)(2,1)S(1)}, u32[]{:S(2)}, u32[]{:S(2)}) %collective-permute-start.29) | collective-permute-done | bytes 65568 | tf_op jit(solution)/shard_map/ppermute | solution.py:87
  262.1 6.4 %collective-permute-done.30 = bf16[8,4096]{1,0:T(8,128)(2,1)S(1)} collective-permute-done((bf16[8,4096]{1,0:T(8,128)(2,1)S(1)}, bf16[8,4096]{1,0:T(8,128)(2,1)S(1)}, u32[]{:S(2)}, u32[]{:S(2)}) %collective-permute-start.30) | collective-permute-done | bytes 65568 | tf_op jit(solution)/shard_map/ppermute | solution.py:87
  268.8 0.8 fusion.18
  269.5 0.8 fusion.12
  271.2 1.4 convolution_convert_fusion
  272.6 55.9 %reduce-scatter.5.cloned.1.call-done = bf16[8,4096]{1,0:T(8,128)(2,1)} async-done(((bf16[128,4096]{1,0:T(8,128)(2,1)}), bf16[8,4096]{1,0:T(8,128)(2,1)}) %reduce-scatter.5.cloned.1.call-update) | async-done | bytes 65552 | tf_op jit(solution)/shard_map/reduce_scatter | solution.py:127
  328.5 0.9 add_bitcast_fusion
  329.4 0.7 maximum_bitcast_fusion
  (106 shorter events, 4.1 us)
Async XLA Ops:
  6.5 102.7 %copy-start = (bf16[1,128,4096]{2,1,0:T(8,128)(2,1)S(1)}, bf16[1,128,4096]{2,1,0:T(8,128)(2,1)}, u32[]{:S(2)}) copy-start(bf16[1,128,4096]{2,1,0:T(8,128)(2,1)} %param.19) | copy-start | bytes 3145732
  6.5 159.6 %reduce-scatter.3.cloned.1.call-start = ((), (), s32[]{:S(2)}) async-start(), calls=%async_computation.2 | async-start | bytes 1114112 | tf_op jit(solution)/shard_map/reduce_scatter | solution.py:127
  8.7 7.5 %collective-permute-start = (bf16[8,4096]{1,0:T(8,128)(2,1)S(1)}, bf16[8,4096]{1,0:T(8,128)(2,1)S(1)}, u32[]{:S(2)}, u32[]{:S(2)}) collective-permute-start(bf16[8,4096]{1,0:T(8,128)(2,1)S(1)} %fusion.24), channel_id=1, source_target_pairs={{0,1},{1,2},{2,3},{3,4},{4,5},{5,6},{6,7},{7,8},{8,9},{9,10},{10,1... | collective-permute-start | bytes 196616 | tf_op jit(solution)/shard_map/ppermute | solution.py:87
  16.2 6.4 %collective-permute-start.1 = (bf16[8,4096]{1,0:T(8,128)(2,1)S(1)}, bf16[8,4096]{1,0:T(8,128)(2,1)S(1)}, u32[]{:S(2)}, u32[]{:S(2)}) collective-permute-start(bf16[8,4096]{1,0:T(8,128)(2,1)S(1)} %collective-permute-done), channel_id=1, source_target_pairs={{0,1},{1,2},{2,3},{3,4},{4,5},{5,6},{6,7},{7,8},{8,9},{9,10},{10,1... | collective-permute-start | bytes 196616 | tf_op jit(solution)/shard_map/ppermute | solution.py:87
  22.6 6.4 %collective-permute-start.2 = (bf16[8,4096]{1,0:T(8,128)(2,1)S(1)}, bf16[8,4096]{1,0:T(8,128)(2,1)S(1)}, u32[]{:S(2)}, u32[]{:S(2)}) collective-permute-start(bf16[8,4096]{1,0:T(8,128)(2,1)S(1)} %collective-permute-done.1), channel_id=1, source_target_pairs={{0,1},{1,2},{2,3},{3,4},{4,5},{5,6},{6,7},{7,8},{8,9},{9,10},{10,1... | collective-permute-start | bytes 196616 | tf_op jit(solution)/shard_map/ppermute | solution.py:87
  28.9 6.4 %collective-permute-start.3 = (bf16[8,4096]{1,0:T(8,128)(2,1)S(1)}, bf16[8,4096]{1,0:T(8,128)(2,1)S(1)}, u32[]{:S(2)}, u32[]{:S(2)}) collective-permute-start(bf16[8,4096]{1,0:T(8,128)(2,1)S(1)} %collective-permute-done.2), channel_id=1, source_target_pairs={{0,1},{1,2},{2,3},{3,4},{4,5},{5,6},{6,7},{7,8},{8,9},{9,10},{10,1... | collective-permute-start | bytes 196616 | tf_op jit(solution)/shard_map/ppermute | solution.py:87
  35.3 6.4 %collective-permute-start.4 = (bf16[8,4096]{1,0:T(8,128)(2,1)S(1)}, bf16[8,4096]{1,0:T(8,128)(2,1)S(1)}, u32[]{:S(2)}, u32[]{:S(2)}) collective-permute-start(bf16[8,4096]{1,0:T(8,128)(2,1)S(1)} %collective-permute-done.3), channel_id=1, source_target_pairs={{0,1},{1,2},{2,3},{3,4},{4,5},{5,6},{6,7},{7,8},{8,9},{9,10},{10,1... | collective-permute-start | bytes 196616 | tf_op jit(solution)/shard_map/ppermute | solution.py:87
  41.7 6.4 %collective-permute-start.5 = (bf16[8,4096]{1,0:T(8,128)(2,1)S(1)}, bf16[8,4096]{1,0:T(8,128)(2,1)S(1)}, u32[]{:S(2)}, u32[]{:S(2)}) collective-permute-start(bf16[8,4096]{1,0:T(8,128)(2,1)S(1)} %collective-permute-done.4), channel_id=1, source_target_pairs={{0,1},{1,2},{2,3},{3,4},{4,5},{5,6},{6,7},{7,8},{8,9},{9,10},{10,1... | collective-permute-start | bytes 196616 | tf_op jit(solution)/shard_map/ppermute | solution.py:87
  48.1 6.4 %collective-permute-start.6 = (bf16[8,4096]{1,0:T(8,128)(2,1)S(1)}, bf16[8,4096]{1,0:T(8,128)(2,1)S(1)}, u32[]{:S(2)}, u32[]{:S(2)}) collective-permute-start(bf16[8,4096]{1,0:T(8,128)(2,1)S(1)} %collective-permute-done.5), channel_id=1, source_target_pairs={{0,1},{1,2},{2,3},{3,4},{4,5},{5,6},{6,7},{7,8},{8,9},{9,10},{10,1... | collective-permute-start | bytes 196616 | tf_op jit(solution)/shard_map/ppermute | solution.py:87
  54.5 6.4 %collective-permute-start.7 = (bf16[8,4096]{1,0:T(8,128)(2,1)S(1)}, bf16[8,4096]{1,0:T(8,128)(2,1)S(1)}, u32[]{:S(2)}, u32[]{:S(2)}) collective-permute-start(bf16[8,4096]{1,0:T(8,128)(2,1)S(1)} %collective-permute-done.6), channel_id=1, source_target_pairs={{0,1},{1,2},{2,3},{3,4},{4,5},{5,6},{6,7},{7,8},{8,9},{9,10},{10,1... | collective-permute-start | bytes 196616 | tf_op jit(solution)/shard_map/ppermute | solution.py:87
  60.9 6.4 %collective-permute-start.8 = (bf16[8,4096]{1,0:T(8,128)(2,1)S(1)}, bf16[8,4096]{1,0:T(8,128)(2,1)S(1)}, u32[]{:S(2)}, u32[]{:S(2)}) collective-permute-start(bf16[8,4096]{1,0:T(8,128)(2,1)S(1)} %collective-permute-done.7), channel_id=1, source_target_pairs={{0,1},{1,2},{2,3},{3,4},{4,5},{5,6},{6,7},{7,8},{8,9},{9,10},{10,1... | collective-permute-start | bytes 196616 | tf_op jit(solution)/shard_map/ppermute | solution.py:87
  67.3 6.4 %collective-permute-start.9 = (bf16[8,4096]{1,0:T(8,128)(2,1)S(1)}, bf16[8,4096]{1,0:T(8,128)(2,1)S(1)}, u32[]{:S(2)}, u32[]{:S(2)}) collective-permute-start(bf16[8,4096]{1,0:T(8,128)(2,1)S(1)} %collective-permute-done.8), channel_id=1, source_target_pairs={{0,1},{1,2},{2,3},{3,4},{4,5},{5,6},{6,7},{7,8},{8,9},{9,10},{10,1... | collective-permute-start | bytes 196616 | tf_op jit(solution)/shard_map/ppermute | solution.py:87
  73.7 6.4 %collective-permute-start.10 = (bf16[8,4096]{1,0:T(8,128)(2,1)S(1)}, bf16[8,4096]{1,0:T(8,128)(2,1)S(1)}, u32[]{:S(2)}, u32[]{:S(2)}) collective-permute-start(bf16[8,4096]{1,0:T(8,128)(2,1)S(1)} %collective-permute-done.9), channel_id=1, source_target_pairs={{0,1},{1,2},{2,3},{3,4},{4,5},{5,6},{6,7},{7,8},{8,9},{9,10},{10,1... | collective-permute-start | bytes 196616 | tf_op jit(solution)/shard_map/ppermute | solution.py:87
  80.0 6.4 %collective-permute-start.11 = (bf16[8,4096]{1,0:T(8,128)(2,1)S(1)}, bf16[8,4096]{1,0:T(8,128)(2,1)S(1)}, u32[]{:S(2)}, u32[]{:S(2)}) collective-permute-start(bf16[8,4096]{1,0:T(8,128)(2,1)S(1)} %collective-permute-done.10), channel_id=1, source_target_pairs={{0,1},{1,2},{2,3},{3,4},{4,5},{5,6},{6,7},{7,8},{8,9},{9,10},{10,1... | collective-permute-start | bytes 196616 | tf_op jit(solution)/shard_map/ppermute | solution.py:87
  86.4 6.4 %collective-permute-start.12 = (bf16[8,4096]{1,0:T(8,128)(2,1)S(1)}, bf16[8,4096]{1,0:T(8,128)(2,1)S(1)}, u32[]{:S(2)}, u32[]{:S(2)}) collective-permute-start(bf16[8,4096]{1,0:T(8,128)(2,1)S(1)} %collective-permute-done.11), channel_id=1, source_target_pairs={{0,1},{1,2},{2,3},{3,4},{4,5},{5,6},{6,7},{7,8},{8,9},{9,10},{10,1... | collective-permute-start | bytes 196616 | tf_op jit(solution)/shard_map/ppermute | solution.py:87
  92.8 6.4 %collective-permute-start.13 = (bf16[8,4096]{1,0:T(8,128)(2,1)S(1)}, bf16[8,4096]{1,0:T(8,128)(2,1)S(1)}, u32[]{:S(2)}, u32[]{:S(2)}) collective-permute-start(bf16[8,4096]{1,0:T(8,128)(2,1)S(1)} %collective-permute-done.12), channel_id=1, source_target_pairs={{0,1},{1,2},{2,3},{3,4},{4,5},{5,6},{6,7},{7,8},{8,9},{9,10},{10,1... | collective-permute-start | bytes 196616 | tf_op jit(solution)/shard_map/ppermute | solution.py:87
  94.3 11.5 %copy-start.1 = (f32[1,8,4096]{2,1,0:T(8,128)S(1)}, f32[1,8,4096]{2,1,0:T(8,128)}, u32[]{:S(2)}) copy-start(f32[1,8,4096]{2,1,0:T(8,128)} %param.11) | copy-start | bytes 393220
  94.3 11.5 %copy-start.2 = (f32[1,4096]{1,0:T(1,128)S(1)}, f32[1,4096]{1,0:T(1,128)}, u32[]{:S(2)}) copy-start(f32[1,4096]{1,0:T(1,128)} %param.16) | copy-start | bytes 49156
  99.2 6.4 %collective-permute-start.14 = (bf16[8,4096]{1,0:T(8,128)(2,1)S(1)}, bf16[8,4096]{1,0:T(8,128)(2,1)S(1)}, u32[]{:S(2)}, u32[]{:S(2)}) collective-permute-start(bf16[8,4096]{1,0:T(8,128)(2,1)S(1)} %collective-permute-done.13), channel_id=1, source_target_pairs={{0,1},{1,2},{2,3},{3,4},{4,5},{5,6},{6,7},{7,8},{8,9},{9,10},{10,1... | collective-permute-start | bytes 196616 | tf_op jit(solution)/shard_map/ppermute | solution.py:87
  105.6 1.2 copy-start.5
  110.7 0.7 copy-start.7
  110.7 61.6 %copy-start.3 = (bf16[1,8,4096]{2,1,0:T(8,128)(2,1)S(1)}, bf16[1,8,4096]{2,1,0:T(8,128)(2,1)}, u32[]{:S(2)}) copy-start(bf16[1,8,4096]{2,1,0:T(8,128)(2,1)} %param.12) | copy-start | bytes 196612
  110.7 61.6 %copy-start.4 = (bf16[1,8,4096]{2,1,0:T(8,128)(2,1)S(1)}, bf16[1,8,4096]{2,1,0:T(8,128)(2,1)}, u32[]{:S(2)}) copy-start(bf16[1,8,4096]{2,1,0:T(8,128)(2,1)} %param.13) | copy-start | bytes 196612
  110.7 217.8 %reduce-scatter.5.cloned.1.call-start = ((), (), s32[]{:S(2)}) async-start(), calls=%async_computation.3 | async-start | bytes 1114112 | tf_op jit(solution)/shard_map/reduce_scatter | solution.py:127
  167.0 5.3 %collective-permute-start.15 = (bf16[8,4096]{1,0:T(8,128)(2,1)S(1)}, bf16[8,4096]{1,0:T(8,128)(2,1)S(1)}, u32[]{:S(2)}, u32[]{:S(2)}) collective-permute-start(bf16[8,4096]{1,0:T(8,128)(2,1)S(1)} %get-tuple-element.9), channel_id=1, source_target_pairs={{0,16},{1,17},{2,18},{3,19},{4,20},{5,21},{6,22},{7,23},{8,24},{9,... | collective-permute-start | bytes 196616 | tf_op jit(solution)/shard_map/ppermute | solution.py:15
  172.6 6.4 %collective-permute-start.16 = (bf16[8,4096]{1,0:T(8,128)(2,1)S(1)}, bf16[8,4096]{1,0:T(8,128)(2,1)S(1)}, u32[]{:S(2)}, u32[]{:S(2)}) collective-permute-start(bf16[8,4096]{1,0:T(8,128)(2,1)S(1)} %multiply_convert_fusion), channel_id=1, source_target_pairs={{0,1},{1,2},{2,3},{3,4},{4,5},{5,6},{6,7},{7,8},{8,9},{9,10},{10,1... | collective-permute-start | bytes 196616 | tf_op jit(solution)/shard_map/ppermute | solution.py:87
  179.1 6.4 %collective-permute-start.17 = (bf16[8,4096]{1,0:T(8,128)(2,1)S(1)}, bf16[8,4096]{1,0:T(8,128)(2,1)S(1)}, u32[]{:S(2)}, u32[]{:S(2)}) collective-permute-start(bf16[8,4096]{1,0:T(8,128)(2,1)S(1)} %collective-permute-done.16), channel_id=1, source_target_pairs={{0,1},{1,2},{2,3},{3,4},{4,5},{5,6},{6,7},{7,8},{8,9},{9,10},{10,1... | collective-permute-start | bytes 196616 | tf_op jit(solution)/shard_map/ppermute | solution.py:87
  185.5 6.4 %collective-permute-start.18 = (bf16[8,4096]{1,0:T(8,128)(2,1)S(1)}, bf16[8,4096]{1,0:T(8,128)(2,1)S(1)}, u32[]{:S(2)}, u32[]{:S(2)}) collective-permute-start(bf16[8,4096]{1,0:T(8,128)(2,1)S(1)} %collective-permute-done.17), channel_id=1, source_target_pairs={{0,1},{1,2},{2,3},{3,4},{4,5},{5,6},{6,7},{7,8},{8,9},{9,10},{10,1... | collective-permute-start | bytes 196616 | tf_op jit(solution)/shard_map/ppermute | solution.py:87
  191.9 6.4 %collective-permute-start.19 = (bf16[8,4096]{1,0:T(8,128)(2,1)S(1)}, bf16[8,4096]{1,0:T(8,128)(2,1)S(1)}, u32[]{:S(2)}, u32[]{:S(2)}) collective-permute-start(bf16[8,4096]{1,0:T(8,128)(2,1)S(1)} %collective-permute-done.18), channel_id=1, source_target_pairs={{0,1},{1,2},{2,3},{3,4},{4,5},{5,6},{6,7},{7,8},{8,9},{9,10},{10,1... | collective-permute-start | bytes 196616 | tf_op jit(solution)/shard_map/ppermute | solution.py:87
  198.3 6.4 %collective-permute-start.20 = (bf16[8,4096]{1,0:T(8,128)(2,1)S(1)}, bf16[8,4096]{1,0:T(8,128)(2,1)S(1)}, u32[]{:S(2)}, u32[]{:S(2)}) collective-permute-start(bf16[8,4096]{1,0:T(8,128)(2,1)S(1)} %collective-permute-done.19), channel_id=1, source_target_pairs={{0,1},{1,2},{2,3},{3,4},{4,5},{5,6},{6,7},{7,8},{8,9},{9,10},{10,1... | collective-permute-start | bytes 196616 | tf_op jit(solution)/shard_map/ppermute | solution.py:87
  204.6 6.4 %collective-permute-start.21 = (bf16[8,4096]{1,0:T(8,128)(2,1)S(1)}, bf16[8,4096]{1,0:T(8,128)(2,1)S(1)}, u32[]{:S(2)}, u32[]{:S(2)}) collective-permute-start(bf16[8,4096]{1,0:T(8,128)(2,1)S(1)} %collective-permute-done.20), channel_id=1, source_target_pairs={{0,1},{1,2},{2,3},{3,4},{4,5},{5,6},{6,7},{7,8},{8,9},{9,10},{10,1... | collective-permute-start | bytes 196616 | tf_op jit(solution)/shard_map/ppermute | solution.py:87
  211.0 6.4 %collective-permute-start.22 = (bf16[8,4096]{1,0:T(8,128)(2,1)S(1)}, bf16[8,4096]{1,0:T(8,128)(2,1)S(1)}, u32[]{:S(2)}, u32[]{:S(2)}) collective-permute-start(bf16[8,4096]{1,0:T(8,128)(2,1)S(1)} %collective-permute-done.21), channel_id=1, source_target_pairs={{0,1},{1,2},{2,3},{3,4},{4,5},{5,6},{6,7},{7,8},{8,9},{9,10},{10,1... | collective-permute-start | bytes 196616 | tf_op jit(solution)/shard_map/ppermute | solution.py:87
  217.4 6.4 %collective-permute-start.23 = (bf16[8,4096]{1,0:T(8,128)(2,1)S(1)}, bf16[8,4096]{1,0:T(8,128)(2,1)S(1)}, u32[]{:S(2)}, u32[]{:S(2)}) collective-permute-start(bf16[8,4096]{1,0:T(8,128)(2,1)S(1)} %collective-permute-done.22), channel_id=1, source_target_pairs={{0,1},{1,2},{2,3},{3,4},{4,5},{5,6},{6,7},{7,8},{8,9},{9,10},{10,1... | collective-permute-start | bytes 196616 | tf_op jit(solution)/shard_map/ppermute | solution.py:87
  223.8 6.4 %collective-permute-start.24 = (bf16[8,4096]{1,0:T(8,128)(2,1)S(1)}, bf16[8,4096]{1,0:T(8,128)(2,1)S(1)}, u32[]{:S(2)}, u32[]{:S(2)}) collective-permute-start(bf16[8,4096]{1,0:T(8,128)(2,1)S(1)} %collective-permute-done.23), channel_id=1, source_target_pairs={{0,1},{1,2},{2,3},{3,4},{4,5},{5,6},{6,7},{7,8},{8,9},{9,10},{10,1... | collective-permute-start | bytes 196616 | tf_op jit(solution)/shard_map/ppermute | solution.py:87
  230.2 6.4 %collective-permute-start.25 = (bf16[8,4096]{1,0:T(8,128)(2,1)S(1)}, bf16[8,4096]{1,0:T(8,128)(2,1)S(1)}, u32[]{:S(2)}, u32[]{:S(2)}) collective-permute-start(bf16[8,4096]{1,0:T(8,128)(2,1)S(1)} %collective-permute-done.24), channel_id=1, source_target_pairs={{0,1},{1,2},{2,3},{3,4},{4,5},{5,6},{6,7},{7,8},{8,9},{9,10},{10,1... | collective-permute-start | bytes 196616 | tf_op jit(solution)/shard_map/ppermute | solution.py:87
  236.6 6.4 %collective-permute-start.26 = (bf16[8,4096]{1,0:T(8,128)(2,1)S(1)}, bf16[8,4096]{1,0:T(8,128)(2,1)S(1)}, u32[]{:S(2)}, u32[]{:S(2)}) collective-permute-start(bf16[8,4096]{1,0:T(8,128)(2,1)S(1)} %collective-permute-done.25), channel_id=1, source_target_pairs={{0,1},{1,2},{2,3},{3,4},{4,5},{5,6},{6,7},{7,8},{8,9},{9,10},{10,1... | collective-permute-start | bytes 196616 | tf_op jit(solution)/shard_map/ppermute | solution.py:87
  243.0 6.4 %collective-permute-start.27 = (bf16[8,4096]{1,0:T(8,128)(2,1)S(1)}, bf16[8,4096]{1,0:T(8,128)(2,1)S(1)}, u32[]{:S(2)}, u32[]{:S(2)}) collective-permute-start(bf16[8,4096]{1,0:T(8,128)(2,1)S(1)} %collective-permute-done.26), channel_id=1, source_target_pairs={{0,1},{1,2},{2,3},{3,4},{4,5},{5,6},{6,7},{7,8},{8,9},{9,10},{10,1... | collective-permute-start | bytes 196616 | tf_op jit(solution)/shard_map/ppermute | solution.py:87
  249.4 6.4 %collective-permute-start.28 = (bf16[8,4096]{1,0:T(8,128)(2,1)S(1)}, bf16[8,4096]{1,0:T(8,128)(2,1)S(1)}, u32[]{:S(2)}, u32[]{:S(2)}) collective-permute-start(bf16[8,4096]{1,0:T(8,128)(2,1)S(1)} %collective-permute-done.27), channel_id=1, source_target_pairs={{0,1},{1,2},{2,3},{3,4},{4,5},{5,6},{6,7},{7,8},{8,9},{9,10},{10,1... | collective-permute-start | bytes 196616 | tf_op jit(solution)/shard_map/ppermute | solution.py:87
  255.7 6.4 %collective-permute-start.29 = (bf16[8,4096]{1,0:T(8,128)(2,1)S(1)}, bf16[8,4096]{1,0:T(8,128)(2,1)S(1)}, u32[]{:S(2)}, u32[]{:S(2)}) collective-permute-start(bf16[8,4096]{1,0:T(8,128)(2,1)S(1)} %collective-permute-done.28), channel_id=1, source_target_pairs={{0,1},{1,2},{2,3},{3,4},{4,5},{5,6},{6,7},{7,8},{8,9},{9,10},{10,1... | collective-permute-start | bytes 196616 | tf_op jit(solution)/shard_map/ppermute | solution.py:87
  262.1 6.4 %collective-permute-start.30 = (bf16[8,4096]{1,0:T(8,128)(2,1)S(1)}, bf16[8,4096]{1,0:T(8,128)(2,1)S(1)}, u32[]{:S(2)}, u32[]{:S(2)}) collective-permute-start(bf16[8,4096]{1,0:T(8,128)(2,1)S(1)} %collective-permute-done.29), channel_id=1, source_target_pairs={{0,1},{1,2},{2,3},{3,4},{4,5},{5,6},{6,7},{7,8},{8,9},{9,10},{10,1... | collective-permute-start | bytes 196616 | tf_op jit(solution)/shard_map/ppermute | solution.py:87
  262.1 6.6 %copy-start.6 = (bf16[1,4096,128]{2,1,0:T(8,128)(2,1)S(1)}, bf16[1,4096,128]{2,1,0:T(8,128)(2,1)}, u32[]{:S(2)}) copy-start(bf16[1,4096,128]{2,1,0:T(8,128)(2,1)} %param.18) | copy-start | bytes 3145732
Sparse Core Ops, SparseCore 0:
  110.8 55.2 reduce-scatter.2
  272.7 55.7 reduce-scatter.4
